TPU v7x, 32 devices: a whole 2x2x4 slice. The times are simulated.
32 devices in a mesh: gx: 4 (over z), gy: 2 (over x), gz: 4 (over y, core).
Axes of the slice: x: 2, y: 2, z: 4, core: 2. Of those that a mesh axis runs over, the one named last changes fastest.
Arguments:
- old_slots: bfloat16 [4, 2, 32, 4096], P('gx', 'gy', 'gz'), may hold values from -6 to 6
- old_ids: int32 [4, 2, 32], P('gx', 'gy', 'gz'), may hold values from -1 to 31, as said below
- old_owner: int32 [4, 2, 32], P('gx', 'gy'), may hold values from 0 to 3, as said below
- coefficient: float32 [64, 32, 512], P('gx', 'gy', 'gz'), may hold values from 0.2 to 5
Outputs:
- solution: float32 [64, 32, 512], P('gx', 'gy', 'gz')
Inputs may be any that keep to these rules, and one draw needn't show every extreme that they name: old_owner[a, c, b] is the index along gz of the device that held box b of box column (a, c) before the move; no device holds more than 8 boxes of a column and some device holds exactly 8; no device holds more than 2 of the 8 boxes with one value of b // 8, and that bound is reached. old_ids[a, c, g * 8 + q] is the box held in slot q of device g of box column (a, c), or -1 for an empty slot; it agrees with old_owner and each box stands in exactly one slot.
All inputs are finite; a program needn't handle non-finite values.
Results may differ from a plain program's by a relative error of at most 0.0003.
Values may be sent and summed in bfloat16 or wider, within the bound.
No kernel may reach another device: no remote copies, remote signals or barrier semaphores. Data moves between devices by JAX's collectives and lax.ppermute only.
A program may use at most 64 MiB of HBM per device.

v0:
```python
import jax
import jax.numpy as jnp
from jax import lax
from jax.sharding import PartitionSpec as P

BOX = 16
NB = 8
SEND = 2
SWEEPS = 2


def with_halo(cells, sides, width):
    for axis, dim in sides:
        count = lax.axis_size(axis)
        ends = count - 1
        head = lax.slice_in_dim(cells, 0, width, axis=dim)
        tail = lax.slice_in_dim(cells, cells.shape[dim] - width, cells.shape[dim], axis=dim)
        cells = jnp.concatenate(
            [
                lax.ppermute(tail, axis, [(i, (i + 1) % count) for i in range(ends)]),
                cells,
                lax.ppermute(head, axis, [((i + 1) % count, i) for i in range(ends)]),
            ],
            axis=dim,
        )
    return cells


def rims(values, depth):
    return with_halo(values, (("gx", 0), ("gy", 1), ("gz", 2)), depth)


def inner(padded):
    return padded[1:-1, 1:-1, 1:-1]


def operator_parts(padded):
    face_first = 0.5 * (padded[:-1, 1:-1, 1:-1] + padded[1:, 1:-1, 1:-1])
    face_second = 0.5 * (padded[1:-1, :-1, 1:-1] + padded[1:-1, 1:, 1:-1])
    face_third = 0.5 * (padded[1:-1, 1:-1, :-1] + padded[1:-1, 1:-1, 1:])
    diagonal = (
        face_first[:-1]
        + face_first[1:]
        + face_second[:, :-1]
        + face_second[:, 1:]
        + face_third[:, :, :-1]
        + face_third[:, :, 1:]
    )
    return (face_first, face_second, face_third, diagonal)


def neighbours(padded, stencil):
    face_first, face_second, face_third, diagonal = stencil
    summed = face_first[:-1] * padded[:-2, 1:-1, 1:-1] + face_first[1:] * padded[2:, 1:-1, 1:-1]
    summed = (
        summed
        + face_second[:, :-1] * padded[1:-1, :-2, 1:-1]
        + face_second[:, 1:] * padded[1:-1, 2:, 1:-1]
    )
    summed = (
        summed
        + face_third[:, :, :-1] * padded[1:-1, 1:-1, :-2]
        + face_third[:, :, 1:] * padded[1:-1, 1:-1, 2:]
    )
    return summed


def red_cells(shape, margin):
    index_first = lax.broadcasted_iota(jnp.int32, shape, 0)
    index_second = lax.broadcasted_iota(jnp.int32, shape, 1)
    index_third = lax.broadcasted_iota(jnp.int32, shape, 2)
    return (index_first + index_second + index_third + margin) % 2 == 0


def relax(padded, source, stencil, factor, chosen):
    fresh = (factor * source + neighbours(padded, stencil)) / stencil[3]
    return jnp.where(chosen, fresh, inner(padded))


def apply_operator(values, stencil, factor):
    return (stencil[3] * values - neighbours(rims(values, 1), stencil)) / factor


def sweep_thin(values, source, stencil, factor, red_mask, starting):
    if starting:
        values = jnp.where(red_mask, factor * source / stencil[3], 0.0)
    else:
        values = relax(rims(values, 1), source, stencil, factor, red_mask)
    return relax(rims(values, 1), source, stencil, factor, jnp.logical_not(red_mask))


def smooth_thin(values, source, stencil, factor, starting):
    red_mask = red_cells(source.shape, 0)
    for counter in range(SWEEPS):
        values = sweep_thin(values, source, stencil, factor, red_mask, starting and counter == 0)
    return values


def sweep_deep(
    values, source_rim, stencil_rim, stencil_block, factor, red_rim, black_block, starting
):
    if starting:
        coloured = jnp.where(red_rim, factor * source_rim / stencil_rim[3], 0.0)
    else:
        coloured = relax(rims(values, 2), source_rim, stencil_rim, factor, red_rim)
    return relax(coloured, inner(source_rim), stencil_block, factor, black_block)


def coarsen(values):
    extent_first, extent_second, extent_third = values.shape
    grouped = values.reshape(extent_first // 2, 2, extent_second // 2, 2, extent_third // 2, 2)
    return grouped.mean(axis=(1, 3, 5))


def refine(values):
    return jnp.repeat(jnp.repeat(jnp.repeat(values, 2, axis=0), 2, axis=1), 2, axis=2)


def dot_pair(first_term, second_term):
    return lax.psum((first_term, second_term), ("gx", "gy", "gz"))


def bottom_solve(rhs_low, stencil, factor):
    image_low = apply_operator(rhs_low, stencil, factor)
    norm_rhs, along_rhs = dot_pair(jnp.sum(rhs_low * rhs_low), jnp.sum(rhs_low * image_low))
    alpha_step = norm_rhs / along_rhs
    rest_low = rhs_low - alpha_step * image_low
    turned = apply_operator(rest_low, stencil, factor)
    turned_rest, turned_norm = dot_pair(jnp.sum(turned * rest_low), jnp.sum(turned * turned))
    omega_step = turned_rest / turned_norm
    return alpha_step * rhs_low + omega_step * rest_low


def move_boxes(old_slots, old_ids, old_owner):
    slot_rows = old_slots.reshape(old_slots.shape[2], old_slots.shape[3])
    slot_ids = old_ids.reshape(-1)
    owner_map = old_owner.reshape(-1)
    groups = lax.axis_size("gz")
    my_index = lax.axis_index("gz")
    capacity = slot_ids.shape[0]
    filled = slot_ids >= 0
    target = jnp.where(filled, slot_ids // NB, -1)
    earlier = (
        (target[None, :] == target[:, None])
        & (slot_ids[None, :] < slot_ids[:, None])
        & filled[None, :]
    )
    ranking = jnp.sum(earlier.astype(jnp.int32), axis=1)
    send_row = jnp.where(filled, target * SEND + ranking, -1)
    picker = lax.broadcasted_iota(jnp.int32, (groups * SEND, capacity), 0) == send_row[None, :]
    outgoing = jnp.dot(
        picker.astype(jnp.bfloat16), slot_rows, preferred_element_type=jnp.float32
    ).astype(jnp.bfloat16)
    incoming = lax.all_to_all(outgoing, "gz", split_axis=0, concat_axis=0, tiled=True).astype(
        jnp.float32
    )
    arriving = lax.dynamic_slice_in_dim(owner_map, my_index * NB, NB)
    later_index = lax.broadcasted_iota(jnp.int32, (NB, NB), 0)
    before = (arriving[None, :] == arriving[:, None]) & (
        lax.broadcasted_iota(jnp.int32, (NB, NB), 1) < later_index
    )
    order_within = jnp.sum(before.astype(jnp.int32), axis=1)
    chosen_boxes = jnp.take(incoming, arriving * SEND + order_within, axis=0)
    stacked = chosen_boxes.reshape(NB, BOX, BOX, BOX).transpose(1, 2, 0, 3)
    return stacked.reshape(BOX, BOX, NB * BOX)


def per_device(old_slots, old_ids, old_owner, coefficient):
    source_fine = move_boxes(old_slots, old_ids, old_owner)
    coefficient_rim = rims(coefficient, 2)
    inside = inner(coefficient_rim) > 0.0
    face_first, face_second, face_third, diagonal = operator_parts(coefficient_rim)
    stencil_rim = (face_first, face_second, face_third, jnp.where(inside, diagonal, 1.0))
    stencil_fine = (inner(face_first), inner(face_second), inner(face_third), inner(diagonal))
    source_rim = rims(source_fine, 1)
    red_rim = jnp.logical_and(red_cells(inside.shape, 1), inside)
    black_fine = jnp.logical_not(red_cells(source_fine.shape, 0))

    def smooth_fine(values, starting):
        for counter in range(SWEEPS):
            values = sweep_deep(
                values,
                source_rim,
                stencil_rim,
                stencil_fine,
                1.0,
                red_rim,
                black_fine,
                starting and counter == 0,
            )
        return values

    fine_values = smooth_fine(jnp.zeros_like(source_fine), True)
    residual_fine = source_fine - apply_operator(fine_values, stencil_fine, 1.0)
    coefficient_mid = coarsen(coefficient)
    stencil_mid = operator_parts(rims(coefficient_mid, 1))
    source_mid = coarsen(residual_fine)
    middle_values = smooth_thin(jnp.zeros_like(source_mid), source_mid, stencil_mid, 4.0, True)
    residual_mid = source_mid - apply_operator(middle_values, stencil_mid, 4.0)
    coefficient_low = coarsen(coefficient_mid)
    stencil_low = operator_parts(rims(coefficient_low, 1))
    bottom_values = bottom_solve(coarsen(residual_mid), stencil_low, 16.0)
    middle_values = smooth_thin(
        middle_values + refine(bottom_values), source_mid, stencil_mid, 4.0, False
    )
    return smooth_fine(fine_values + refine(middle_values), False)


def solution(mesh):
    in_specs = (
        P("gx", "gy", "gz", None),
        P("gx", "gy", "gz"),
        P("gx", "gy", None),
        P("gx", "gy", "gz"),
    )
    out_specs = P("gx", "gy", "gz")
    return jax.shard_map(
        per_device, mesh=mesh, in_specs=in_specs, out_specs=out_specs, check_vma=False
    )
```

profile of v0, /device:TPU:1, one launch (start us, length us, event | category | flops | bytes accessed | tf_op | source)
XLA Modules:
  0.0 550.7 jit_solution(12764030653669933789)
XLA Ops:
  2.1 4.6 collective-permute-start
  10.5 4.2 all-to-all-start
  14.7 10.6 %reshape.184 = f32[8,2,8,2,64,2]{5,4,3,2,1,0:T(8,128)} reshape(f32[16,16,128]{2,1,0:T(8,128)} %param.7) | data formatting | bytes 262144 | tf_op jit(solution)/shard_map/reshape | solution.py:111
  25.3 4.0 reduce_sum.96
  29.9 4.2 collective-permute-start.24
  35.9 3.1 collective-permute-start.2
  40.4 3.1 collective-permute-done.3
  43.7 5.3 collective-permute-start.4
  52.1 4.4 collective-permute-done.5
  58.6 4.3 collective-permute-start.6
  64.9 3.1 collective-permute-done.7
  73.9 4.6 collective-permute-start.10
  81.4 4.4 collective-permute-done.11
  94.6 4.0 collective-permute-start.14
  103.3 4.0 collective-permute-start.16
  110.4 4.4 collective-permute-done.17
  117.0 4.3 collective-permute-start.18
  129.8 3.0 collective-permute-done.21
  133.0 4.7 collective-permute-start.22
  140.5 4.4 collective-permute-done.23
  145.4 9.8 %reshape.183 = f32[8,2,8,2,64,2]{5,4,3,2,1,0:T(8,128)} reshape(f32[16,16,128]{2,1,0:T(8,128)S(1)} %fusion.55) | data formatting | bytes 262144 | tf_op jit(solution)/shard_map/reshape | solution.py:111
  155.2 4.0 reduce_sum.95
  159.4 4.3 collective-permute-start.30
  170.7 3.1 collective-permute-done.33
  173.9 4.6 collective-permute-start.34
  180.4 3.8 collective-permute-done.35
  193.7 3.1 collective-permute-done.39
  196.8 4.7 collective-permute-start.40
  203.5 3.8 collective-permute-done.41
  219.3 4.7 collective-permute-start.46
  229.9 3.3 collective-permute-start.48
  237.6 3.7 collective-permute-start.50
  245.8 6.5 %collective-permute-start.52 = (f32[10,10,1]{2,1,0:T(8,128)S(1)}, f32[10,10,1]{2,1,0:T(8,128)S(1)}, u32[]{:S(2)}, u32[]{:S(2)}) collective-permute-start(f32[10,10,1]{2,1,0:T(8,128)S(1)} %get-tuple-element.61), channel_id=1, source_target_pairs={{0,1},{1,2},{2,3},{4,5},{5,6},{6,7},{8,9},{9,10},{10,11},{12,13},{... | collective-permute-start | bytes 1208 | tf_op jit(solution)/shard_map/ppermute | solution.py:20
  254.2 3.8 collective-permute-done.53
  259.4 4.3 collective-permute-start.60
  275.2 4.8 collective-permute-start.64
  285.9 37.9 %all-reduce.1 = (f32[]{:T(128)}, f32[]{:T(128)}) all-reduce(f32[]{:T(128)} %get-tuple-element.8, f32[]{:T(128)} %get-tuple-element.7), channel_id=1, replica_groups=mesh['gx'=4,'gy'=2,'gz'=4] {'gx','gy','gz'}, use_global_device_ids=true, to_apply=%region_6.7 | all-reduce | flops 2 | bytes 16 | tf_op jit(solution)/shard_map/psum | solution.py:120
  331.1 4.3 collective-permute-start.68
  339.9 7.3 %collective-permute-start.70 = (f32[6,6,1]{2,1,0:T(8,128)S(1)}, f32[6,6,1]{2,1,0:T(8,128)S(1)}, u32[]{:S(2)}, u32[]{:S(2)}) collective-permute-start(f32[6,6,1]{2,1,0:T(8,128)S(1)} %get-tuple-element.107), channel_id=1, source_target_pairs={{0,1},{1,2},{2,3},{4,5},{5,6},{6,7},{8,9},{9,10},{10,11},{12,13},{... | collective-permute-start | bytes 440 | tf_op jit(solution)/shard_map/ppermute | solution.py:20
  349.2 3.2 collective-permute-done.71
  353.2 36.6 %all-reduce = (f32[]{:T(128)}, f32[]{:T(128)}) all-reduce(f32[]{:T(128)} %get-tuple-element.6, f32[]{:T(128)} %get-tuple-element.5), channel_id=1, replica_groups=mesh['gx'=4,'gy'=2,'gz'=4] {'gx','gy','gz'}, use_global_device_ids=true, to_apply=%region_11.12 | all-reduce | flops 2 | bytes 16 | tf_op jit(solution)/shard_map/psum | solution.py:120
  398.2 4.3 collective-permute-start.74
  403.8 3.1 collective-permute-done.75
  407.0 7.3 %collective-permute-start.76 = (f32[10,10,1]{2,1,0:T(8,128)S(1)}, f32[10,10,1]{2,1,0:T(8,128)S(1)}, u32[]{:S(2)}, u32[]{:S(2)}) collective-permute-start(f32[10,10,1]{2,1,0:T(8,128)S(1)} %get-tuple-element.59), channel_id=1, source_target_pairs={{0,1},{1,2},{2,3},{4,5},{5,6},{6,7},{8,9},{9,10},{10,11},{12,13},{... | collective-permute-start | bytes 1208 | tf_op jit(solution)/shard_map/ppermute | solution.py:20
  416.3 3.8 collective-permute-done.77
  423.9 3.3 collective-permute-done.79
  429.9 3.1 collective-permute-done.81
  433.1 4.4 collective-permute-start.82
  439.5 3.8 collective-permute-done.83
  443.4 3.6 collective-permute-start.84
  454.1 3.1 collective-permute-done.87
  457.3 4.7 collective-permute-start.88
  464.0 3.8 collective-permute-done.89
  476.6 3.1 collective-permute-done.93
  479.8 4.7 collective-permute-start.94
  486.7 3.6 collective-permute-done.95
  497.7 3.2 collective-permute-done.97
  503.6 3.2 collective-permute-done.99
  507.0 4.7 collective-permute-start.100
  514.8 4.4 collective-permute-done.101
  525.4 3.2 collective-permute-done.103
  531.3 3.2 collective-permute-done.105
  534.7 4.6 collective-permute-start.106
  542.4 4.4 collective-permute-done.107
  (346 shorter events, 204.8 us)
Async XLA Ops:
  0.8 35.1 %collective-permute-start.1 = (f32[2,16,128]{2,1,0:T(8,128)S(1)}, f32[2,16,128]{2,1,0:T(8,128)S(1)}, u32[]{:S(2)}, u32[]{:S(2)}) collective-permute-start(f32[2,16,128]{2,1,0:T(8,128)S(1)} %get-tuple-element.51), channel_id=1, source_target_pairs={{8,0},{16,8},{24,16},{9,1},{17,9},{25,17},{10,2},{18,10},{26,18},{... | collective-permute-start | bytes 49160 | tf_op jit(solution)/shard_map/ppermute | solution.py:22
  2.1 33.7 %collective-permute-start = (f32[2,16,128]{2,1,0:T(8,128)S(1)}, f32[2,16,128]{2,1,0:T(8,128)S(1)}, u32[]{:S(2)}, u32[]{:S(2)}) collective-permute-start(f32[2,16,128]{2,1,0:T(8,128)S(1)} %get-tuple-element.52), channel_id=1, source_target_pairs={{0,8},{8,16},{16,24},{1,9},{9,17},{17,25},{2,10},{10,18},{18,26},{... | collective-permute-start | bytes 49160 | tf_op jit(solution)/shard_map/ppermute | solution.py:20
  10.5 46.4 %all-to-all-start = ((bf16[4,2,4096]{2,1,0:T(2,128)(2,1)}), bf16[4,2,4096]{2,1,0:T(2,128)(2,1)S(1)}, u32[]{:S(2)}, u32[]{:S(2)}) async-start(bf16[4,2,4096]{2,1,0:T(2,128)(2,1)} %all_to_all.6), calls=%async_computation | async-start | bytes 131072 | tf_op jit(solution)/shard_map/all_to_all | solution.py:154
  29.9 61.0 %collective-permute-start.24 = (f32[1,8,64]{2,1,0:T(8,128)}, f32[1,8,64]{2,1,0:T(8,128)}, u32[]{:S(2)}, u32[]{:S(2)}) collective-permute-start(f32[1,8,64]{2,1,0:T(8,128)} %get-tuple-element.105), channel_id=1, source_target_pairs={{0,8},{8,16},{16,24},{1,9},{9,17},{17,25},{2,10},{10,18},{18,26},{... | collective-permute-start | bytes 6152 | tf_op jit(solution)/shard_map/ppermute | solution.py:20
  34.2 56.8 %collective-permute-start.25 = (f32[1,8,64]{2,1,0:T(8,128)}, f32[1,8,64]{2,1,0:T(8,128)}, u32[]{:S(2)}, u32[]{:S(2)}) collective-permute-start(f32[1,8,64]{2,1,0:T(8,128)} %get-tuple-element.106), channel_id=1, source_target_pairs={{8,0},{16,8},{24,16},{9,1},{17,9},{25,17},{10,2},{18,10},{26,18},{... | collective-permute-start | bytes 6152 | tf_op jit(solution)/shard_map/ppermute | solution.py:22
  39.0 4.5 collective-permute-start.3
  43.7 8.4 %collective-permute-start.4 = (f32[20,20,2]{2,1,0:T(8,128)S(1)}, f32[20,20,2]{2,1,0:T(8,128)S(1)}, u32[]{:S(2)}, u32[]{:S(2)}) collective-permute-start(f32[20,20,2]{2,1,0:T(8,128)S(1)} %get-tuple-element.25), channel_id=1, source_target_pairs={{0,1},{1,2},{2,3},{4,5},{5,6},{6,7},{8,9},{9,10},{10,11},{12,13},{... | collective-permute-start | bytes 9608 | tf_op jit(solution)/shard_map/ppermute | solution.py:20
  49.0 7.5 %collective-permute-start.5 = (f32[20,20,2]{2,1,0:T(8,128)S(1)}, f32[20,20,2]{2,1,0:T(8,128)S(1)}, u32[]{:S(2)}, u32[]{:S(2)}) collective-permute-start(f32[20,20,2]{2,1,0:T(8,128)S(1)} %get-tuple-element.26), channel_id=1, source_target_pairs={{1,0},{2,1},{3,2},{5,4},{6,5},{7,6},{9,8},{10,9},{11,10},{13,12},{... | collective-permute-start | bytes 9608 | tf_op jit(solution)/shard_map/ppermute | solution.py:22
  58.6 6.3 %collective-permute-start.6 = (f32[1,16,128]{2,1,0:T(8,128)S(1)}, f32[1,16,128]{2,1,0:T(8,128)S(1)}, u32[]{:S(2)}, u32[]{:S(2)}) collective-permute-start(f32[1,16,128]{2,1,0:T(8,128)S(1)} %slice.1002), channel_id=1, source_target_pairs={{0,8},{8,16},{16,24},{1,9},{9,17},{17,25},{2,10},{10,18},{18,26},{... | collective-permute-start | bytes 24584 | tf_op jit(solution)/shard_map/ppermute | solution.py:20
  73.9 7.5 %collective-permute-start.10 = (f32[18,18,1]{2,1,0:T(8,128)S(1)}, f32[18,18,1]{2,1,0:T(8,128)S(1)}, u32[]{:S(2)}, u32[]{:S(2)}) collective-permute-start(f32[18,18,1]{2,1,0:T(8,128)S(1)} %get-tuple-element.29), channel_id=1, source_target_pairs={{0,1},{1,2},{2,3},{4,5},{5,6},{6,7},{8,9},{9,10},{10,11},{12,13},{... | collective-permute-start | bytes 3896 | tf_op jit(solution)/shard_map/ppermute | solution.py:20
  78.5 7.3 %collective-permute-start.11 = (f32[18,18,1]{2,1,0:T(8,128)S(1)}, f32[18,18,1]{2,1,0:T(8,128)S(1)}, u32[]{:S(2)}, u32[]{:S(2)}) collective-permute-start(f32[18,18,1]{2,1,0:T(8,128)S(1)} %get-tuple-element.30), channel_id=1, source_target_pairs={{1,0},{2,1},{3,2},{5,4},{6,5},{7,6},{9,8},{10,9},{11,10},{13,12},{... | collective-permute-start | bytes 3896 | tf_op jit(solution)/shard_map/ppermute | solution.py:22
  87.0 7.5 %collective-permute-start.12 = (f32[2,16,128]{2,1,0:T(8,128)S(1)}, f32[2,16,128]{2,1,0:T(8,128)S(1)}, u32[]{:S(2)}, u32[]{:S(2)}) collective-permute-start(f32[2,16,128]{2,1,0:T(8,128)S(1)} %get-tuple-element.49), channel_id=1, source_target_pairs={{0,8},{8,16},{16,24},{1,9},{9,17},{17,25},{2,10},{10,18},{18,26},{... | collective-permute-start | bytes 49160 | tf_op jit(solution)/shard_map/ppermute | solution.py:20
  89.7 4.9 collective-permute-start.13
  91.9 17.4 %collective-permute-start.26 = (f32[10,1,64]{2,1,0:T(1,128)S(1)}, f32[10,1,64]{2,1,0:T(1,128)S(1)}, u32[]{:S(2)}, u32[]{:S(2)}) collective-permute-start(f32[10,1,64]{2,1,0:T(1,128)S(1)} %get-tuple-element.87), channel_id=1, source_target_pairs={{0,4},{1,5},{2,6},{3,7},{8,12},{9,13},{10,14},{11,15},{16,20},{17,... | collective-permute-start | bytes 7688 | tf_op jit(solution)/shard_map/ppermute | solution.py:20
  93.2 16.0 %collective-permute-start.27 = (f32[10,1,64]{2,1,0:T(1,128)S(1)}, f32[10,1,64]{2,1,0:T(1,128)S(1)}, u32[]{:S(2)}, u32[]{:S(2)}) collective-permute-start(f32[10,1,64]{2,1,0:T(1,128)S(1)} %get-tuple-element.88), channel_id=1, source_target_pairs={{4,0},{5,1},{6,2},{7,3},{12,8},{13,9},{14,10},{15,11},{20,16},{21,... | collective-permute-start | bytes 7688 | tf_op jit(solution)/shard_map/ppermute | solution.py:22
  94.6 6.1 %collective-permute-start.14 = (f32[20,2,128]{2,1,0:T(2,128)S(1)}, f32[20,2,128]{2,1,0:T(2,128)S(1)}, u32[]{:S(2)}, u32[]{:S(2)}) collective-permute-start(f32[20,2,128]{2,1,0:T(2,128)S(1)} %get-tuple-element.35), channel_id=1, source_target_pairs={{0,4},{1,5},{2,6},{3,7},{8,12},{9,13},{10,14},{11,15},{16,20},{17,... | collective-permute-start | bytes 61448 | tf_op jit(solution)/shard_map/ppermute | solution.py:20
  98.6 4.5 collective-permute-start.15
  103.3 7.1 %collective-permute-start.16 = (f32[20,20,2]{2,1,0:T(8,128)S(1)}, f32[20,20,2]{2,1,0:T(8,128)S(1)}, u32[]{:S(2)}, u32[]{:S(2)}) collective-permute-start(f32[20,20,2]{2,1,0:T(8,128)S(1)} %get-tuple-element.23), channel_id=1, source_target_pairs={{0,1},{1,2},{2,3},{4,5},{5,6},{6,7},{8,9},{9,10},{10,11},{12,13},{... | collective-permute-start | bytes 9608 | tf_op jit(solution)/shard_map/ppermute | solution.py:20
  107.3 7.5 %collective-permute-start.17 = (f32[20,20,2]{2,1,0:T(8,128)S(1)}, f32[20,20,2]{2,1,0:T(8,128)S(1)}, u32[]{:S(2)}, u32[]{:S(2)}) collective-permute-start(f32[20,20,2]{2,1,0:T(8,128)S(1)} %get-tuple-element.24), channel_id=1, source_target_pairs={{1,0},{2,1},{3,2},{5,4},{6,5},{7,6},{9,8},{10,9},{11,10},{13,12},{... | collective-permute-start | bytes 9608 | tf_op jit(solution)/shard_map/ppermute | solution.py:22
  117.0 10.0 %collective-permute-start.18 = (f32[1,16,128]{2,1,0:T(8,128)S(1)}, f32[1,16,128]{2,1,0:T(8,128)S(1)}, u32[]{:S(2)}, u32[]{:S(2)}) collective-permute-start(f32[1,16,128]{2,1,0:T(8,128)S(1)} %get-tuple-element.47), channel_id=1, source_target_pairs={{0,8},{8,16},{16,24},{1,9},{9,17},{17,25},{2,10},{10,18},{18,26},{... | collective-permute-start | bytes 24584 | tf_op jit(solution)/shard_map/ppermute | solution.py:20
  121.3 5.7 %collective-permute-start.19 = (f32[1,16,128]{2,1,0:T(8,128)S(1)}, f32[1,16,128]{2,1,0:T(8,128)S(1)}, u32[]{:S(2)}, u32[]{:S(2)}) collective-permute-start(f32[1,16,128]{2,1,0:T(8,128)S(1)} %get-tuple-element.48), channel_id=1, source_target_pairs={{8,0},{16,8},{24,16},{9,1},{17,9},{25,17},{10,2},{18,10},{26,18},{... | collective-permute-start | bytes 24584 | tf_op jit(solution)/shard_map/ppermute | solution.py:22
  122.7 17.1 %collective-permute-start.28 = (f32[10,10,1]{2,1,0:T(8,128)S(1)}, f32[10,10,1]{2,1,0:T(8,128)S(1)}, u32[]{:S(2)}, u32[]{:S(2)}) collective-permute-start(f32[10,10,1]{2,1,0:T(8,128)S(1)} %get-tuple-element.69), channel_id=1, source_target_pairs={{0,1},{1,2},{2,3},{4,5},{5,6},{6,7},{8,9},{9,10},{10,11},{12,13},{... | collective-permute-start | bytes 1208 | tf_op jit(solution)/shard_map/ppermute | solution.py:20
  124.7 15.1 %collective-permute-start.29 = (f32[10,10,1]{2,1,0:T(8,128)S(1)}, f32[10,10,1]{2,1,0:T(8,128)S(1)}, u32[]{:S(2)}, u32[]{:S(2)}) collective-permute-start(f32[10,10,1]{2,1,0:T(8,128)S(1)} %get-tuple-element.70), channel_id=1, source_target_pairs={{1,0},{2,1},{3,2},{5,4},{6,5},{7,6},{9,8},{10,9},{11,10},{13,12},{... | collective-permute-start | bytes 1208 | tf_op jit(solution)/shard_map/ppermute | solution.py:22
  133.0 7.6 %collective-permute-start.22 = (f32[18,18,1]{2,1,0:T(8,128)S(1)}, f32[18,18,1]{2,1,0:T(8,128)S(1)}, u32[]{:S(2)}, u32[]{:S(2)}) collective-permute-start(f32[18,18,1]{2,1,0:T(8,128)S(1)} %get-tuple-element.27), channel_id=1, source_target_pairs={{0,1},{1,2},{2,3},{4,5},{5,6},{6,7},{8,9},{9,10},{10,11},{12,13},{... | collective-permute-start | bytes 3896 | tf_op jit(solution)/shard_map/ppermute | solution.py:20
  137.7 7.3 %collective-permute-start.23 = (f32[18,18,1]{2,1,0:T(8,128)S(1)}, f32[18,18,1]{2,1,0:T(8,128)S(1)}, u32[]{:S(2)}, u32[]{:S(2)}) collective-permute-start(f32[18,18,1]{2,1,0:T(8,128)S(1)} %get-tuple-element.28), channel_id=1, source_target_pairs={{1,0},{2,1},{3,2},{5,4},{6,5},{7,6},{9,8},{10,9},{11,10},{13,12},{... | collective-permute-start | bytes 3896 | tf_op jit(solution)/shard_map/ppermute | solution.py:22
  159.4 5.6 %collective-permute-start.30 = (f32[1,8,64]{2,1,0:T(8,128)S(1)}, f32[1,8,64]{2,1,0:T(8,128)S(1)}, u32[]{:S(2)}, u32[]{:S(2)}) collective-permute-start(f32[1,8,64]{2,1,0:T(8,128)S(1)} %get-tuple-element.103), channel_id=1, source_target_pairs={{0,8},{8,16},{16,24},{1,9},{9,17},{17,25},{2,10},{10,18},{18,26},{... | collective-permute-start | bytes 6152 | tf_op jit(solution)/shard_map/ppermute | solution.py:20
  173.9 6.5 %collective-permute-start.34 = (f32[10,10,1]{2,1,0:T(8,128)S(1)}, f32[10,10,1]{2,1,0:T(8,128)S(1)}, u32[]{:S(2)}, u32[]{:S(2)}) collective-permute-start(f32[10,10,1]{2,1,0:T(8,128)S(1)} %get-tuple-element.67), channel_id=1, source_target_pairs={{0,1},{1,2},{2,3},{4,5},{5,6},{6,7},{8,9},{9,10},{10,11},{12,13},{... | collective-permute-start | bytes 1208 | tf_op jit(solution)/shard_map/ppermute | solution.py:20
  178.5 5.8 %collective-permute-start.35 = (f32[10,10,1]{2,1,0:T(8,128)S(1)}, f32[10,10,1]{2,1,0:T(8,128)S(1)}, u32[]{:S(2)}, u32[]{:S(2)}) collective-permute-start(f32[10,10,1]{2,1,0:T(8,128)S(1)} %get-tuple-element.68), channel_id=1, source_target_pairs={{1,0},{2,1},{3,2},{5,4},{6,5},{7,6},{9,8},{10,9},{11,10},{13,12},{... | collective-permute-start | bytes 1208 | tf_op jit(solution)/shard_map/ppermute | solution.py:22
  196.8 6.6 %collective-permute-start.40 = (f32[10,10,1]{2,1,0:T(8,128)S(1)}, f32[10,10,1]{2,1,0:T(8,128)S(1)}, u32[]{:S(2)}, u32[]{:S(2)}) collective-permute-start(f32[10,10,1]{2,1,0:T(8,128)S(1)} %get-tuple-element.65), channel_id=1, source_target_pairs={{0,1},{1,2},{2,3},{4,5},{5,6},{6,7},{8,9},{9,10},{10,11},{12,13},{... | collective-permute-start | bytes 1208 | tf_op jit(solution)/shard_map/ppermute | solution.py:20
  201.5 5.8 %collective-permute-start.41 = (f32[10,10,1]{2,1,0:T(8,128)S(1)}, f32[10,10,1]{2,1,0:T(8,128)S(1)}, u32[]{:S(2)}, u32[]{:S(2)}) collective-permute-start(f32[10,10,1]{2,1,0:T(8,128)S(1)} %get-tuple-element.66), channel_id=1, source_target_pairs={{1,0},{2,1},{3,2},{5,4},{6,5},{7,6},{9,8},{10,9},{11,10},{13,12},{... | collective-permute-start | bytes 1208 | tf_op jit(solution)/shard_map/ppermute | solution.py:22
  219.3 9.7 %collective-permute-start.46 = (f32[10,10,1]{2,1,0:T(8,128)S(1)}, f32[10,10,1]{2,1,0:T(8,128)S(1)}, u32[]{:S(2)}, u32[]{:S(2)}) collective-permute-start(f32[10,10,1]{2,1,0:T(8,128)S(1)} %get-tuple-element.63), channel_id=1, source_target_pairs={{0,1},{1,2},{2,3},{4,5},{5,6},{6,7},{8,9},{9,10},{10,11},{12,13},{... | collective-permute-start | bytes 1208 | tf_op jit(solution)/shard_map/ppermute | solution.py:20
  224.0 5.8 %collective-permute-start.47 = (f32[10,10,1]{2,1,0:T(8,128)S(1)}, f32[10,10,1]{2,1,0:T(8,128)S(1)}, u32[]{:S(2)}, u32[]{:S(2)}) collective-permute-start(f32[10,10,1]{2,1,0:T(8,128)S(1)} %get-tuple-element.64), channel_id=1, source_target_pairs={{1,0},{2,1},{3,2},{5,4},{6,5},{7,6},{9,8},{10,9},{11,10},{13,12},{... | collective-permute-start | bytes 1208 | tf_op jit(solution)/shard_map/ppermute | solution.py:22
  226.0 8.6 %collective-permute-start.54 = (f32[1,4,32]{2,1,0:T(4,128)S(1)}, f32[1,4,32]{2,1,0:T(4,128)S(1)}, u32[]{:S(2)}, u32[]{:S(2)}) collective-permute-start(f32[1,4,32]{2,1,0:T(4,128)S(1)} %get-tuple-element.121), channel_id=1, source_target_pairs={{0,8},{8,16},{16,24},{1,9},{9,17},{17,25},{2,10},{10,18},{18,26},{... | collective-permute-start | bytes 1544 | tf_op jit(solution)/shard_map/ppermute | solution.py:20
  227.6 6.9 %collective-permute-start.55 = (f32[1,4,32]{2,1,0:T(4,128)S(1)}, f32[1,4,32]{2,1,0:T(4,128)S(1)}, u32[]{:S(2)}, u32[]{:S(2)}) collective-permute-start(f32[1,4,32]{2,1,0:T(4,128)S(1)} %get-tuple-element.122), channel_id=1, source_target_pairs={{8,0},{16,8},{24,16},{9,1},{17,9},{25,17},{10,2},{18,10},{26,18},{... | collective-permute-start | bytes 1544 | tf_op jit(solution)/shard_map/ppermute | solution.py:22
  229.9 7.3 %collective-permute-start.48 = (f32[1,8,64]{2,1,0:T(8,128)S(1)}, f32[1,8,64]{2,1,0:T(8,128)S(1)}, u32[]{:S(2)}, u32[]{:S(2)}) collective-permute-start(f32[1,8,64]{2,1,0:T(8,128)S(1)} %get-tuple-element.97), channel_id=1, source_target_pairs={{0,8},{8,16},{16,24},{1,9},{9,17},{17,25},{2,10},{10,18},{18,26},{... | collective-permute-start | bytes 6152 | tf_op jit(solution)/shard_map/ppermute | solution.py:20
  234.6 19.6 %collective-permute-start.56 = (f32[6,1,32]{2,1,0:T(1,128)S(1)}, f32[6,1,32]{2,1,0:T(1,128)S(1)}, u32[]{:S(2)}, u32[]{:S(2)}) collective-permute-start(f32[6,1,32]{2,1,0:T(1,128)S(1)} %get-tuple-element.115), channel_id=1, source_target_pairs={{0,4},{1,5},{2,6},{3,7},{8,12},{9,13},{10,14},{11,15},{16,20},{17,... | collective-permute-start | bytes 2312 | tf_op jit(solution)/shard_map/ppermute | solution.py:20
  235.9 18.2 %collective-permute-start.57 = (f32[6,1,32]{2,1,0:T(1,128)S(1)}, f32[6,1,32]{2,1,0:T(1,128)S(1)}, u32[]{:S(2)}, u32[]{:S(2)}) collective-permute-start(f32[6,1,32]{2,1,0:T(1,128)S(1)} %get-tuple-element.116), channel_id=1, source_target_pairs={{4,0},{5,1},{6,2},{7,3},{12,8},{13,9},{14,10},{15,11},{20,16},{21,... | collective-permute-start | bytes 2312 | tf_op jit(solution)/shard_map/ppermute | solution.py:22
  237.6 5.0 collective-permute-start.50
  245.8 8.5 %collective-permute-start.52 = (f32[10,10,1]{2,1,0:T(8,128)S(1)}, f32[10,10,1]{2,1,0:T(8,128)S(1)}, u32[]{:S(2)}, u32[]{:S(2)}) collective-permute-start(f32[10,10,1]{2,1,0:T(8,128)S(1)} %get-tuple-element.61), channel_id=1, source_target_pairs={{0,1},{1,2},{2,3},{4,5},{5,6},{6,7},{8,9},{9,10},{10,11},{12,13},{... | collective-permute-start | bytes 1208 | tf_op jit(solution)/shard_map/ppermute | solution.py:20
  252.2 5.8 %collective-permute-start.53 = (f32[10,10,1]{2,1,0:T(8,128)S(1)}, f32[10,10,1]{2,1,0:T(8,128)S(1)}, u32[]{:S(2)}, u32[]{:S(2)}) collective-permute-start(f32[10,10,1]{2,1,0:T(8,128)S(1)} %get-tuple-element.62), channel_id=1, source_target_pairs={{1,0},{2,1},{3,2},{5,4},{6,5},{7,6},{9,8},{10,9},{11,10},{13,12},{... | collective-permute-start | bytes 1208 | tf_op jit(solution)/shard_map/ppermute | solution.py:22
  259.4 10.0 %collective-permute-start.60 = (f32[1,4,32]{2,1,0:T(4,128)S(1)}, f32[1,4,32]{2,1,0:T(4,128)S(1)}, u32[]{:S(2)}, u32[]{:S(2)}) collective-permute-start(f32[1,4,32]{2,1,0:T(4,128)S(1)} %get-tuple-element.123), channel_id=1, source_target_pairs={{0,8},{8,16},{16,24},{1,9},{9,17},{17,25},{2,10},{10,18},{18,26},{... | collective-permute-start | bytes 1544 | tf_op jit(solution)/shard_map/ppermute | solution.py:20
  263.7 5.7 %collective-permute-start.61 = (f32[1,4,32]{2,1,0:T(4,128)S(1)}, f32[1,4,32]{2,1,0:T(4,128)S(1)}, u32[]{:S(2)}, u32[]{:S(2)}) collective-permute-start(f32[1,4,32]{2,1,0:T(4,128)S(1)} %get-tuple-element.124), channel_id=1, source_target_pairs={{8,0},{16,8},{24,16},{9,1},{17,9},{25,17},{10,2},{18,10},{26,18},{... | collective-permute-start | bytes 1544 | tf_op jit(solution)/shard_map/ppermute | solution.py:22
  265.0 16.9 %collective-permute-start.58 = (f32[6,6,1]{2,1,0:T(8,128)S(1)}, f32[6,6,1]{2,1,0:T(8,128)S(1)}, u32[]{:S(2)}, u32[]{:S(2)}) collective-permute-start(f32[6,6,1]{2,1,0:T(8,128)S(1)} %get-tuple-element.109), channel_id=1, source_target_pairs={{0,1},{1,2},{2,3},{4,5},{5,6},{6,7},{8,9},{9,10},{10,11},{12,13},{... | collective-permute-start | bytes 440 | tf_op jit(solution)/shard_map/ppermute | solution.py:20
  267.2 14.8 %collective-permute-start.59 = (f32[6,6,1]{2,1,0:T(8,128)S(1)}, f32[6,6,1]{2,1,0:T(8,128)S(1)}, u32[]{:S(2)}, u32[]{:S(2)}) collective-permute-start(f32[6,6,1]{2,1,0:T(8,128)S(1)} %get-tuple-element.110), channel_id=1, source_target_pairs={{1,0},{2,1},{3,2},{5,4},{6,5},{7,6},{9,8},{10,9},{11,10},{13,12},{... | collective-permute-start | bytes 440 | tf_op jit(solution)/shard_map/ppermute | solution.py:22
  275.2 7.6 %collective-permute-start.64 = (f32[6,6,1]{2,1,0:T(8,128)S(1)}, f32[6,6,1]{2,1,0:T(8,128)S(1)}, u32[]{:S(2)}, u32[]{:S(2)}) collective-permute-start(f32[6,6,1]{2,1,0:T(8,128)S(1)} %get-tuple-element.111), channel_id=1, source_target_pairs={{0,1},{1,2},{2,3},{4,5},{5,6},{6,7},{8,9},{9,10},{10,11},{12,13},{... | collective-permute-start | bytes 440 | tf_op jit(solution)/shard_map/ppermute | solution.py:20
  280.0 5.1 collective-permute-start.65
  331.1 5.7 %collective-permute-start.68 = (f32[6,1,32]{2,1,0:T(1,128)S(1)}, f32[6,1,32]{2,1,0:T(1,128)S(1)}, u32[]{:S(2)}, u32[]{:S(2)}) collective-permute-start(f32[6,1,32]{2,1,0:T(1,128)S(1)} %get-tuple-element.113), channel_id=1, source_target_pairs={{0,4},{1,5},{2,6},{3,7},{8,12},{9,13},{10,14},{11,15},{16,20},{17,... | collective-permute-start | bytes 2312 | tf_op jit(solution)/shard_map/ppermute | solution.py:20
  339.9 9.3 %collective-permute-start.70 = (f32[6,6,1]{2,1,0:T(8,128)S(1)}, f32[6,6,1]{2,1,0:T(8,128)S(1)}, u32[]{:S(2)}, u32[]{:S(2)}) collective-permute-start(f32[6,6,1]{2,1,0:T(8,128)S(1)} %get-tuple-element.107), channel_id=1, source_target_pairs={{0,1},{1,2},{2,3},{4,5},{5,6},{6,7},{8,9},{9,10},{10,11},{12,13},{... | collective-permute-start | bytes 440 | tf_op jit(solution)/shard_map/ppermute | solution.py:20
  347.3 5.1 collective-permute-start.71
  398.2 5.7 %collective-permute-start.74 = (f32[10,1,64]{2,1,0:T(1,128)S(1)}, f32[10,1,64]{2,1,0:T(1,128)S(1)}, u32[]{:S(2)}, u32[]{:S(2)}) collective-permute-start(f32[10,1,64]{2,1,0:T(1,128)S(1)} %get-tuple-element.77), channel_id=1, source_target_pairs={{0,4},{1,5},{2,6},{3,7},{8,12},{9,13},{10,14},{11,15},{16,20},{17,... | collective-permute-start | bytes 7688 | tf_op jit(solution)/shard_map/ppermute | solution.py:20
  407.0 9.3 %collective-permute-start.76 = (f32[10,10,1]{2,1,0:T(8,128)S(1)}, f32[10,10,1]{2,1,0:T(8,128)S(1)}, u32[]{:S(2)}, u32[]{:S(2)}) collective-permute-start(f32[10,10,1]{2,1,0:T(8,128)S(1)} %get-tuple-element.59), channel_id=1, source_target_pairs={{0,1},{1,2},{2,3},{4,5},{5,6},{6,7},{8,9},{9,10},{10,11},{12,13},{... | collective-permute-start | bytes 1208 | tf_op jit(solution)/shard_map/ppermute | solution.py:20
  414.3 5.8 %collective-permute-start.77 = (f32[10,10,1]{2,1,0:T(8,128)S(1)}, f32[10,10,1]{2,1,0:T(8,128)S(1)}, u32[]{:S(2)}, u32[]{:S(2)}) collective-permute-start(f32[10,10,1]{2,1,0:T(8,128)S(1)} %get-tuple-element.60), channel_id=1, source_target_pairs={{1,0},{2,1},{3,2},{5,4},{6,5},{7,6},{9,8},{10,9},{11,10},{13,12},{... | collective-permute-start | bytes 1208 | tf_op jit(solution)/shard_map/ppermute | solution.py:22
  422.6 4.6 collective-permute-start.79
  433.1 6.4 %collective-permute-start.82 = (f32[10,10,1]{2,1,0:T(8,128)S(1)}, f32[10,10,1]{2,1,0:T(8,128)S(1)}, u32[]{:S(2)}, u32[]{:S(2)}) collective-permute-start(f32[10,10,1]{2,1,0:T(8,128)S(1)} %get-tuple-element.57), channel_id=1, source_target_pairs={{0,1},{1,2},{2,3},{4,5},{5,6},{6,7},{8,9},{9,10},{10,11},{12,13},{... | collective-permute-start | bytes 1208 | tf_op jit(solution)/shard_map/ppermute | solution.py:20
  437.5 5.8 %collective-permute-start.83 = (f32[10,10,1]{2,1,0:T(8,128)S(1)}, f32[10,10,1]{2,1,0:T(8,128)S(1)}, u32[]{:S(2)}, u32[]{:S(2)}) collective-permute-start(f32[10,10,1]{2,1,0:T(8,128)S(1)} %get-tuple-element.58), channel_id=1, source_target_pairs={{1,0},{2,1},{3,2},{5,4},{6,5},{7,6},{9,8},{10,9},{11,10},{13,12},{... | collective-permute-start | bytes 1208 | tf_op jit(solution)/shard_map/ppermute | solution.py:22
  443.4 4.9 collective-permute-start.84
  457.3 6.6 %collective-permute-start.88 = (f32[10,10,1]{2,1,0:T(8,128)S(1)}, f32[10,10,1]{2,1,0:T(8,128)S(1)}, u32[]{:S(2)}, u32[]{:S(2)}) collective-permute-start(f32[10,10,1]{2,1,0:T(8,128)S(1)} %get-tuple-element.55), channel_id=1, source_target_pairs={{0,1},{1,2},{2,3},{4,5},{5,6},{6,7},{8,9},{9,10},{10,11},{12,13},{... | collective-permute-start | bytes 1208 | tf_op jit(solution)/shard_map/ppermute | solution.py:20
  462.0 5.8 %collective-permute-start.89 = (f32[10,10,1]{2,1,0:T(8,128)S(1)}, f32[10,10,1]{2,1,0:T(8,128)S(1)}, u32[]{:S(2)}, u32[]{:S(2)}) collective-permute-start(f32[10,10,1]{2,1,0:T(8,128)S(1)} %get-tuple-element.56), channel_id=1, source_target_pairs={{1,0},{2,1},{3,2},{5,4},{6,5},{7,6},{9,8},{10,9},{11,10},{13,12},{... | collective-permute-start | bytes 1208 | tf_op jit(solution)/shard_map/ppermute | solution.py:22
  479.8 6.9 %collective-permute-start.94 = (f32[10,10,1]{2,1,0:T(8,128)S(1)}, f32[10,10,1]{2,1,0:T(8,128)S(1)}, u32[]{:S(2)}, u32[]{:S(2)}) collective-permute-start(f32[10,10,1]{2,1,0:T(8,128)S(1)} %get-tuple-element.53), channel_id=1, source_target_pairs={{0,1},{1,2},{2,3},{4,5},{5,6},{6,7},{8,9},{9,10},{10,11},{12,13},{... | collective-permute-start | bytes 1208 | tf_op jit(solution)/shard_map/ppermute | solution.py:20
  484.5 5.8 %collective-permute-start.95 = (f32[10,10,1]{2,1,0:T(8,128)S(1)}, f32[10,10,1]{2,1,0:T(8,128)S(1)}, u32[]{:S(2)}, u32[]{:S(2)}) collective-permute-start(f32[10,10,1]{2,1,0:T(8,128)S(1)} %get-tuple-element.54), channel_id=1, source_target_pairs={{1,0},{2,1},{3,2},{5,4},{6,5},{7,6},{9,8},{10,9},{11,10},{13,12},{... | collective-permute-start | bytes 1208 | tf_op jit(solution)/shard_map/ppermute | solution.py:22
  507.0 7.8 %collective-permute-start.100 = (f32[20,20,2]{2,1,0:T(8,128)S(1)}, f32[20,20,2]{2,1,0:T(8,128)S(1)}, u32[]{:S(2)}, u32[]{:S(2)}) collective-permute-start(f32[20,20,2]{2,1,0:T(8,128)S(1)} %get-tuple-element.21), channel_id=1, source_target_pairs={{0,1},{1,2},{2,3},{4,5},{5,6},{6,7},{8,9},{9,10},{10,11},{12,13},{... | collective-permute-start | bytes 9608 | tf_op jit(solution)/shard_map/ppermute | solution.py:20
  511.7 7.5 %collective-permute-start.101 = (f32[20,20,2]{2,1,0:T(8,128)S(1)}, f32[20,20,2]{2,1,0:T(8,128)S(1)}, u32[]{:S(2)}, u32[]{:S(2)}) collective-permute-start(f32[20,20,2]{2,1,0:T(8,128)S(1)} %get-tuple-element.22), channel_id=1, source_target_pairs={{1,0},{2,1},{3,2},{5,4},{6,5},{7,6},{9,8},{10,9},{11,10},{13,12},{... | collective-permute-start | bytes 9608 | tf_op jit(solution)/shard_map/ppermute | solution.py:22
  534.7 7.7 %collective-permute-start.106 = (f32[20,20,2]{2,1,0:T(8,128)S(1)}, f32[20,20,2]{2,1,0:T(8,128)S(1)}, u32[]{:S(2)}, u32[]{:S(2)}) collective-permute-start(f32[20,20,2]{2,1,0:T(8,128)S(1)} %get-tuple-element.19), channel_id=1, source_target_pairs={{0,1},{1,2},{2,3},{4,5},{5,6},{6,7},{8,9},{9,10},{10,11},{12,13},{... | collective-permute-start | bytes 9608 | tf_op jit(solution)/shard_map/ppermute | solution.py:20
  539.3 7.5 %collective-permute-start.107 = (f32[20,20,2]{2,1,0:T(8,128)S(1)}, f32[20,20,2]{2,1,0:T(8,128)S(1)}, u32[]{:S(2)}, u32[]{:S(2)}) collective-permute-start(f32[20,20,2]{2,1,0:T(8,128)S(1)} %get-tuple-element.20), channel_id=1, source_target_pairs={{1,0},{2,1},{3,2},{5,4},{6,5},{7,6},{9,8},{10,9},{11,10},{13,12},{... | collective-permute-start | bytes 9608 | tf_op jit(solution)/shard_map/ppermute | solution.py:22
  (62 other events, 1047.8 us)
where the time goes:
time: 554 us; the launch traced here: 551 us
  starting transfers between devices  262 us (47%)
  waiting for transfers between devices  145 us (26%)
  blocking collectives  74.6 us (13%)
  other arithmetic  32.8 us (6%)
  local copies, waits for them, and re-layouts  31.5 us (6%)
    ppermute x54, starting transfers between devices, with_halo(): lax.ppermute(tail, axis, [(i, (i + 1) % count) for i in range(ends)])  175 us
    ppermute x54, waiting for transfers between devices, with_halo(): lax.ppermute(head, axis, [((i + 1) % count, i) for i in range(ends)])  140 us
    ppermute x54, starting transfers between devices, with_halo(): lax.ppermute(head, axis, [((i + 1) % count, i) for i in range(ends)])  82.2 us
    psum x2, blocking collectives, dot_pair(): return lax.psum((first_term, second_term), ('gx', 'gy', 'gz'))  74.6 us
    reshape x3, local copies, waits for them, and re-layouts, coarsen(): values.reshape(extent_first // 2, 2, extent_second // 2, 2, extent_third...  21.5 us
  transfers between devices with their start and end apart: 109, of which 50 were waited for; matrix products, arithmetic and copies ran while one was open for 5% of the time, Pallas kernels for 0%

commit v1 on v0

--- a/solution.py
+++ b/solution.py
@@ -117,7 +117,13 @@
 
 
 def dot_pair(first_term, second_term):
-    return lax.psum((first_term, second_term), ("gx", "gy", "gz"))
+
+    def object_balance(local_array, chip_axis, device_axis):
+        y = lax.psum(local_array, axis_name=chip_axis)
+        local_out = lax.psum(y, axis_name=device_axis)
+        return local_out
+
+    return object_balance((first_term, second_term), ("gy", "gz"), "gx")
 
 
 def bottom_solve(rhs_low, stencil, factor):

time: 554 us -> 513 us (0.926)
  blocking collectives: 74.6 us -> 38 us
    psum x2 -> x4, blocking collectives: 74.6 us -> 38 us  [the longest x2 20.3 us: object_balance(): y = lax.psum(local_array, axis_name=chip_axis)]
  transfers between devices with their start and end apart: 109 -> 109, of which waited for: 50 -> 50; matrix products, arithmetic and copies ran while one was open for 5% -> 6% of each run, Pallas kernels for 0% -> 0%
where the time goes in v1:
time: 513 us; the launch traced here: 510 us
  starting transfers between devices  258 us (50%)
  waiting for transfers between devices  145 us (28%)
  blocking collectives  38 us (7%)
  other arithmetic  32.9 us (6%)
  local copies, waits for them, and re-layouts  31.6 us (6%)
    ppermute x54, starting transfers between devices, with_halo(): lax.ppermute(tail, axis, [(i, (i + 1) % count) for i in range(ends)])  171 us
    ppermute x54, waiting for transfers between devices, with_halo(): lax.ppermute(head, axis, [((i + 1) % count, i) for i in range(ends)])  139 us
    ppermute x54, starting transfers between devices, with_halo(): lax.ppermute(head, axis, [((i + 1) % count, i) for i in range(ends)])  82.3 us
    reshape x3, local copies, waits for them, and re-layouts, coarsen(): values.reshape(extent_first // 2, 2, extent_second // 2, 2, extent_third...  21.5 us
    psum x2, blocking collectives, object_balance(): y = lax.psum(local_array, axis_name=chip_axis)  20.3 us
    psum x2, blocking collectives, object_balance(): local_out = lax.psum(y, axis_name=device_axis)  17.7 us
  transfers between devices with their start and end apart: 109, of which 50 were waited for; matrix products, arithmetic and copies ran while one was open for 6% of the time, Pallas kernels for 0%

profile of v1, /device:TPU:1, one launch (start us, length us, event | category | flops | bytes accessed | tf_op | source)
XLA Modules:
  0.0 509.8 jit_solution(7640483992801324631)
XLA Ops:
  2.1 4.6 collective-permute-start
  10.5 4.2 all-to-all-start
  14.7 10.6 %reshape.184 = f32[8,2,8,2,64,2]{5,4,3,2,1,0:T(8,128)} reshape(f32[16,16,128]{2,1,0:T(8,128)} %param.7) | data formatting | bytes 262144 | tf_op jit(solution)/shard_map/reshape | solution.py:111
  25.3 4.0 reduce_sum.96
  30.0 4.2 collective-permute-start.24
  35.9 3.1 collective-permute-start.2
  40.4 3.1 collective-permute-done.3
  43.7 5.3 %collective-permute-start.4 = (f32[20,20,2]{2,1,0:T(8,128)S(1)}, f32[20,20,2]{2,1,0:T(8,128)S(1)}, u32[]{:S(2)}, u32[]{:S(2)}) collective-permute-start(f32[20,20,2]{2,1,0:T(8,128)S(1)} %get-tuple-element.29), channel_id=1, source_target_pairs={{0,1},{1,2},{2,3},{4,5},{5,6},{6,7},{8,9},{9,10},{10,11},{12,13},{... | collective-permute-start | bytes 9608 | tf_op jit(solution)/shard_map/ppermute | solution.py:20
  52.1 4.4 collective-permute-done.5
  58.6 4.3 collective-permute-start.6
  64.9 3.1 collective-permute-done.7
  74.0 4.6 collective-permute-start.10
  81.4 4.4 collective-permute-done.11
  94.6 4.0 collective-permute-start.14
  103.3 4.0 collective-permute-start.16
  110.4 4.4 collective-permute-done.17
  117.0 4.3 collective-permute-start.18
  129.8 3.0 collective-permute-done.21
  133.0 4.7 collective-permute-start.22
  140.6 4.4 collective-permute-done.23
  145.5 9.8 %reshape.183 = f32[8,2,8,2,64,2]{5,4,3,2,1,0:T(8,128)} reshape(f32[16,16,128]{2,1,0:T(8,128)S(1)} %fusion.55) | data formatting | bytes 262144 | tf_op jit(solution)/shard_map/reshape | solution.py:111
  155.2 4.1 reduce_sum.95
  159.4 4.3 collective-permute-start.30
  165.0 3.0 collective-permute-done.31
  170.7 3.1 collective-permute-done.33
  173.9 4.6 collective-permute-start.34
  180.5 3.8 collective-permute-done.35
  193.7 3.1 collective-permute-done.39
  196.9 4.7 collective-permute-start.40
  203.5 3.8 collective-permute-done.41
  219.4 4.7 collective-permute-start.46
  230.0 3.3 collective-permute-start.48
  237.6 3.7 collective-permute-start.50
  245.8 6.5 %collective-permute-start.52 = (f32[10,10,1]{2,1,0:T(8,128)S(1)}, f32[10,10,1]{2,1,0:T(8,128)S(1)}, u32[]{:S(2)}, u32[]{:S(2)}) collective-permute-start(f32[10,10,1]{2,1,0:T(8,128)S(1)} %get-tuple-element.65), channel_id=1, source_target_pairs={{0,1},{1,2},{2,3},{4,5},{5,6},{6,7},{8,9},{9,10},{10,11},{12,13},{... | collective-permute-start | bytes 1208 | tf_op jit(solution)/shard_map/ppermute | solution.py:20
  254.3 3.8 collective-permute-done.53
  259.4 4.3 collective-permute-start.60
  275.3 4.8 collective-permute-start.64
  286.0 10.1 %all-reduce.1 = (f32[]{:T(128)}, f32[]{:T(128)}) all-reduce(f32[]{:T(128)} %get-tuple-element.8, f32[]{:T(128)} %get-tuple-element.7), channel_id=1, replica_groups=mesh['gx'=4,'gy'=2,'gz'=4] {'gy','gz'}, use_global_device_ids=true, to_apply=%region_6.7 | all-reduce | flops 2 | bytes 16 | tf_op jit(solution)/shard_map/psum | solution.py:122
  296.1 9.9 %all-reduce.3 = (f32[]{:T(128)}, f32[]{:T(128)}) all-reduce(f32[]{:T(128)} %get-tuple-element.11, f32[]{:T(128)} %get-tuple-element.12), channel_id=1, replica_groups=mesh['gx'=4,'gy'=2,'gz'=4] {'gx'}, use_global_device_ids=true, to_apply=%region_7.8 | all-reduce | flops 2 | bytes 16 | tf_op jit(solution)/shard_map/psum | solution.py:123
  319.8 7.6 %collective-permute-start.70 = (f32[6,6,1]{2,1,0:T(8,128)S(1)}, f32[6,6,1]{2,1,0:T(8,128)S(1)}, u32[]{:S(2)}, u32[]{:S(2)}) collective-permute-start(f32[6,6,1]{2,1,0:T(8,128)S(1)} %get-tuple-element.111), channel_id=1, source_target_pairs={{0,1},{1,2},{2,3},{4,5},{5,6},{6,7},{8,9},{9,10},{10,11},{12,13},{... | collective-permute-start | bytes 440 | tf_op jit(solution)/shard_map/ppermute | solution.py:20
  329.3 3.2 collective-permute-done.71
  333.3 10.1 %all-reduce = (f32[]{:T(128)}, f32[]{:T(128)}) all-reduce(f32[]{:T(128)} %get-tuple-element.6, f32[]{:T(128)} %get-tuple-element.5), channel_id=1, replica_groups=mesh['gx'=4,'gy'=2,'gz'=4] {'gy','gz'}, use_global_device_ids=true, to_apply=%region_13.14 | all-reduce | flops 2 | bytes 16 | tf_op jit(solution)/shard_map/psum | solution.py:122
  343.5 7.8 %all-reduce.2 = (f32[]{:T(128)}, f32[]{:T(128)}) all-reduce(f32[]{:T(128)} %get-tuple-element.9, f32[]{:T(128)} %get-tuple-element.10), channel_id=1, replica_groups=mesh['gx'=4,'gy'=2,'gz'=4] {'gx'}, use_global_device_ids=true, to_apply=%region_14.15 | all-reduce | flops 2 | bytes 16 | tf_op jit(solution)/shard_map/psum | solution.py:123
  357.0 3.0 collective-permute-done.73
  364.0 3.1 collective-permute-done.75
  367.2 7.9 %collective-permute-start.76 = (f32[10,10,1]{2,1,0:T(8,128)S(1)}, f32[10,10,1]{2,1,0:T(8,128)S(1)}, u32[]{:S(2)}, u32[]{:S(2)}) collective-permute-start(f32[10,10,1]{2,1,0:T(8,128)S(1)} %get-tuple-element.63), channel_id=1, source_target_pairs={{0,1},{1,2},{2,3},{4,5},{5,6},{6,7},{8,9},{9,10},{10,11},{12,13},{... | collective-permute-start | bytes 1208 | tf_op jit(solution)/shard_map/ppermute | solution.py:20
  377.0 3.8 collective-permute-done.77
  383.9 3.0 collective-permute-done.79
  389.7 3.1 collective-permute-done.81
  392.8 4.7 collective-permute-start.82
  399.5 3.8 collective-permute-done.83
  413.3 3.1 collective-permute-done.87
  416.4 4.7 collective-permute-start.88
  423.1 3.8 collective-permute-done.89
  435.8 3.1 collective-permute-done.93
  438.9 4.7 collective-permute-start.94
  445.6 3.8 collective-permute-done.95
  456.8 3.2 collective-permute-done.97
  466.1 4.7 collective-permute-start.100
  473.9 4.4 collective-permute-done.101
  484.6 3.2 collective-permute-done.103
  490.4 3.2 collective-permute-done.105
  493.8 4.6 collective-permute-start.106
  501.6 4.4 collective-permute-done.107
  (348 shorter events, 209.3 us)
Async XLA Ops:
  0.8 35.1 %collective-permute-start.1 = (f32[2,16,128]{2,1,0:T(8,128)S(1)}, f32[2,16,128]{2,1,0:T(8,128)S(1)}, u32[]{:S(2)}, u32[]{:S(2)}) collective-permute-start(f32[2,16,128]{2,1,0:T(8,128)S(1)} %get-tuple-element.55), channel_id=1, source_target_pairs={{8,0},{16,8},{24,16},{9,1},{17,9},{25,17},{10,2},{18,10},{26,18},{... | collective-permute-start | bytes 49160 | tf_op jit(solution)/shard_map/ppermute | solution.py:22
  2.1 33.8 %collective-permute-start = (f32[2,16,128]{2,1,0:T(8,128)S(1)}, f32[2,16,128]{2,1,0:T(8,128)S(1)}, u32[]{:S(2)}, u32[]{:S(2)}) collective-permute-start(f32[2,16,128]{2,1,0:T(8,128)S(1)} %get-tuple-element.56), channel_id=1, source_target_pairs={{0,8},{8,16},{16,24},{1,9},{9,17},{17,25},{2,10},{10,18},{18,26},{... | collective-permute-start | bytes 49160 | tf_op jit(solution)/shard_map/ppermute | solution.py:20
  10.5 46.4 %all-to-all-start = ((bf16[4,2,4096]{2,1,0:T(2,128)(2,1)}), bf16[4,2,4096]{2,1,0:T(2,128)(2,1)S(1)}, u32[]{:S(2)}, u32[]{:S(2)}) async-start(bf16[4,2,4096]{2,1,0:T(2,128)(2,1)} %all_to_all.6), calls=%async_computation | async-start | bytes 131072 | tf_op jit(solution)/shard_map/all_to_all | solution.py:160
  30.0 61.0 %collective-permute-start.24 = (f32[1,8,64]{2,1,0:T(8,128)}, f32[1,8,64]{2,1,0:T(8,128)}, u32[]{:S(2)}, u32[]{:S(2)}) collective-permute-start(f32[1,8,64]{2,1,0:T(8,128)} %get-tuple-element.109), channel_id=1, source_target_pairs={{0,8},{8,16},{16,24},{1,9},{9,17},{17,25},{2,10},{10,18},{18,26},{... | collective-permute-start | bytes 6152 | tf_op jit(solution)/shard_map/ppermute | solution.py:20
  34.2 56.8 %collective-permute-start.25 = (f32[1,8,64]{2,1,0:T(8,128)}, f32[1,8,64]{2,1,0:T(8,128)}, u32[]{:S(2)}, u32[]{:S(2)}) collective-permute-start(f32[1,8,64]{2,1,0:T(8,128)} %get-tuple-element.110), channel_id=1, source_target_pairs={{8,0},{16,8},{24,16},{9,1},{17,9},{25,17},{10,2},{18,10},{26,18},{... | collective-permute-start | bytes 6152 | tf_op jit(solution)/shard_map/ppermute | solution.py:22
  35.9 4.5 collective-permute-start.2
  39.0 4.5 collective-permute-start.3
  43.7 8.4 %collective-permute-start.4 = (f32[20,20,2]{2,1,0:T(8,128)S(1)}, f32[20,20,2]{2,1,0:T(8,128)S(1)}, u32[]{:S(2)}, u32[]{:S(2)}) collective-permute-start(f32[20,20,2]{2,1,0:T(8,128)S(1)} %get-tuple-element.29), channel_id=1, source_target_pairs={{0,1},{1,2},{2,3},{4,5},{5,6},{6,7},{8,9},{9,10},{10,11},{12,13},{... | collective-permute-start | bytes 9608 | tf_op jit(solution)/shard_map/ppermute | solution.py:20
  49.0 7.5 %collective-permute-start.5 = (f32[20,20,2]{2,1,0:T(8,128)S(1)}, f32[20,20,2]{2,1,0:T(8,128)S(1)}, u32[]{:S(2)}, u32[]{:S(2)}) collective-permute-start(f32[20,20,2]{2,1,0:T(8,128)S(1)} %get-tuple-element.30), channel_id=1, source_target_pairs={{1,0},{2,1},{3,2},{5,4},{6,5},{7,6},{9,8},{10,9},{11,10},{13,12},{... | collective-permute-start | bytes 9608 | tf_op jit(solution)/shard_map/ppermute | solution.py:22
  58.6 6.3 %collective-permute-start.6 = (f32[1,16,128]{2,1,0:T(8,128)S(1)}, f32[1,16,128]{2,1,0:T(8,128)S(1)}, u32[]{:S(2)}, u32[]{:S(2)}) collective-permute-start(f32[1,16,128]{2,1,0:T(8,128)S(1)} %slice.1002), channel_id=1, source_target_pairs={{0,8},{8,16},{16,24},{1,9},{9,17},{17,25},{2,10},{10,18},{18,26},{... | collective-permute-start | bytes 24584 | tf_op jit(solution)/shard_map/ppermute | solution.py:20
  74.0 7.5 %collective-permute-start.10 = (f32[18,18,1]{2,1,0:T(8,128)S(1)}, f32[18,18,1]{2,1,0:T(8,128)S(1)}, u32[]{:S(2)}, u32[]{:S(2)}) collective-permute-start(f32[18,18,1]{2,1,0:T(8,128)S(1)} %get-tuple-element.33), channel_id=1, source_target_pairs={{0,1},{1,2},{2,3},{4,5},{5,6},{6,7},{8,9},{9,10},{10,11},{12,13},{... | collective-permute-start | bytes 3896 | tf_op jit(solution)/shard_map/ppermute | solution.py:20
  78.6 7.3 %collective-permute-start.11 = (f32[18,18,1]{2,1,0:T(8,128)S(1)}, f32[18,18,1]{2,1,0:T(8,128)S(1)}, u32[]{:S(2)}, u32[]{:S(2)}) collective-permute-start(f32[18,18,1]{2,1,0:T(8,128)S(1)} %get-tuple-element.34), channel_id=1, source_target_pairs={{1,0},{2,1},{3,2},{5,4},{6,5},{7,6},{9,8},{10,9},{11,10},{13,12},{... | collective-permute-start | bytes 3896 | tf_op jit(solution)/shard_map/ppermute | solution.py:22
  87.1 7.5 %collective-permute-start.12 = (f32[2,16,128]{2,1,0:T(8,128)S(1)}, f32[2,16,128]{2,1,0:T(8,128)S(1)}, u32[]{:S(2)}, u32[]{:S(2)}) collective-permute-start(f32[2,16,128]{2,1,0:T(8,128)S(1)} %get-tuple-element.53), channel_id=1, source_target_pairs={{0,8},{8,16},{16,24},{1,9},{9,17},{17,25},{2,10},{10,18},{18,26},{... | collective-permute-start | bytes 49160 | tf_op jit(solution)/shard_map/ppermute | solution.py:20
  89.7 4.9 collective-permute-start.13
  91.9 17.4 %collective-permute-start.26 = (f32[10,1,64]{2,1,0:T(1,128)S(1)}, f32[10,1,64]{2,1,0:T(1,128)S(1)}, u32[]{:S(2)}, u32[]{:S(2)}) collective-permute-start(f32[10,1,64]{2,1,0:T(1,128)S(1)} %get-tuple-element.91), channel_id=1, source_target_pairs={{0,4},{1,5},{2,6},{3,7},{8,12},{9,13},{10,14},{11,15},{16,20},{17,... | collective-permute-start | bytes 7688 | tf_op jit(solution)/shard_map/ppermute | solution.py:20
  93.3 16.0 %collective-permute-start.27 = (f32[10,1,64]{2,1,0:T(1,128)S(1)}, f32[10,1,64]{2,1,0:T(1,128)S(1)}, u32[]{:S(2)}, u32[]{:S(2)}) collective-permute-start(f32[10,1,64]{2,1,0:T(1,128)S(1)} %get-tuple-element.92), channel_id=1, source_target_pairs={{4,0},{5,1},{6,2},{7,3},{12,8},{13,9},{14,10},{15,11},{20,16},{21,... | collective-permute-start | bytes 7688 | tf_op jit(solution)/shard_map/ppermute | solution.py:22
  94.6 6.1 %collective-permute-start.14 = (f32[20,2,128]{2,1,0:T(2,128)S(1)}, f32[20,2,128]{2,1,0:T(2,128)S(1)}, u32[]{:S(2)}, u32[]{:S(2)}) collective-permute-start(f32[20,2,128]{2,1,0:T(2,128)S(1)} %get-tuple-element.39), channel_id=1, source_target_pairs={{0,4},{1,5},{2,6},{3,7},{8,12},{9,13},{10,14},{11,15},{16,20},{17,... | collective-permute-start | bytes 61448 | tf_op jit(solution)/shard_map/ppermute | solution.py:20
  98.6 4.5 collective-permute-start.15
  103.3 7.1 %collective-permute-start.16 = (f32[20,20,2]{2,1,0:T(8,128)S(1)}, f32[20,20,2]{2,1,0:T(8,128)S(1)}, u32[]{:S(2)}, u32[]{:S(2)}) collective-permute-start(f32[20,20,2]{2,1,0:T(8,128)S(1)} %get-tuple-element.27), channel_id=1, source_target_pairs={{0,1},{1,2},{2,3},{4,5},{5,6},{6,7},{8,9},{9,10},{10,11},{12,13},{... | collective-permute-start | bytes 9608 | tf_op jit(solution)/shard_map/ppermute | solution.py:20
  107.3 7.5 %collective-permute-start.17 = (f32[20,20,2]{2,1,0:T(8,128)S(1)}, f32[20,20,2]{2,1,0:T(8,128)S(1)}, u32[]{:S(2)}, u32[]{:S(2)}) collective-permute-start(f32[20,20,2]{2,1,0:T(8,128)S(1)} %get-tuple-element.28), channel_id=1, source_target_pairs={{1,0},{2,1},{3,2},{5,4},{6,5},{7,6},{9,8},{10,9},{11,10},{13,12},{... | collective-permute-start | bytes 9608 | tf_op jit(solution)/shard_map/ppermute | solution.py:22
  117.0 10.0 %collective-permute-start.18 = (f32[1,16,128]{2,1,0:T(8,128)S(1)}, f32[1,16,128]{2,1,0:T(8,128)S(1)}, u32[]{:S(2)}, u32[]{:S(2)}) collective-permute-start(f32[1,16,128]{2,1,0:T(8,128)S(1)} %get-tuple-element.51), channel_id=1, source_target_pairs={{0,8},{8,16},{16,24},{1,9},{9,17},{17,25},{2,10},{10,18},{18,26},{... | collective-permute-start | bytes 24584 | tf_op jit(solution)/shard_map/ppermute | solution.py:20
  121.3 5.7 %collective-permute-start.19 = (f32[1,16,128]{2,1,0:T(8,128)S(1)}, f32[1,16,128]{2,1,0:T(8,128)S(1)}, u32[]{:S(2)}, u32[]{:S(2)}) collective-permute-start(f32[1,16,128]{2,1,0:T(8,128)S(1)} %get-tuple-element.52), channel_id=1, source_target_pairs={{8,0},{16,8},{24,16},{9,1},{17,9},{25,17},{10,2},{18,10},{26,18},{... | collective-permute-start | bytes 24584 | tf_op jit(solution)/shard_map/ppermute | solution.py:22
  122.7 17.1 %collective-permute-start.28 = (f32[10,10,1]{2,1,0:T(8,128)S(1)}, f32[10,10,1]{2,1,0:T(8,128)S(1)}, u32[]{:S(2)}, u32[]{:S(2)}) collective-permute-start(f32[10,10,1]{2,1,0:T(8,128)S(1)} %get-tuple-element.73), channel_id=1, source_target_pairs={{0,1},{1,2},{2,3},{4,5},{5,6},{6,7},{8,9},{9,10},{10,11},{12,13},{... | collective-permute-start | bytes 1208 | tf_op jit(solution)/shard_map/ppermute | solution.py:20
  124.7 15.1 %collective-permute-start.29 = (f32[10,10,1]{2,1,0:T(8,128)S(1)}, f32[10,10,1]{2,1,0:T(8,128)S(1)}, u32[]{:S(2)}, u32[]{:S(2)}) collective-permute-start(f32[10,10,1]{2,1,0:T(8,128)S(1)} %get-tuple-element.74), channel_id=1, source_target_pairs={{1,0},{2,1},{3,2},{5,4},{6,5},{7,6},{9,8},{10,9},{11,10},{13,12},{... | collective-permute-start | bytes 1208 | tf_op jit(solution)/shard_map/ppermute | solution.py:22
  133.0 7.6 %collective-permute-start.22 = (f32[18,18,1]{2,1,0:T(8,128)S(1)}, f32[18,18,1]{2,1,0:T(8,128)S(1)}, u32[]{:S(2)}, u32[]{:S(2)}) collective-permute-start(f32[18,18,1]{2,1,0:T(8,128)S(1)} %get-tuple-element.31), channel_id=1, source_target_pairs={{0,1},{1,2},{2,3},{4,5},{5,6},{6,7},{8,9},{9,10},{10,11},{12,13},{... | collective-permute-start | bytes 3896 | tf_op jit(solution)/shard_map/ppermute | solution.py:20
  137.7 7.3 %collective-permute-start.23 = (f32[18,18,1]{2,1,0:T(8,128)S(1)}, f32[18,18,1]{2,1,0:T(8,128)S(1)}, u32[]{:S(2)}, u32[]{:S(2)}) collective-permute-start(f32[18,18,1]{2,1,0:T(8,128)S(1)} %get-tuple-element.32), channel_id=1, source_target_pairs={{1,0},{2,1},{3,2},{5,4},{6,5},{7,6},{9,8},{10,9},{11,10},{13,12},{... | collective-permute-start | bytes 3896 | tf_op jit(solution)/shard_map/ppermute | solution.py:22
  159.4 5.6 %collective-permute-start.30 = (f32[1,8,64]{2,1,0:T(8,128)S(1)}, f32[1,8,64]{2,1,0:T(8,128)S(1)}, u32[]{:S(2)}, u32[]{:S(2)}) collective-permute-start(f32[1,8,64]{2,1,0:T(8,128)S(1)} %get-tuple-element.107), channel_id=1, source_target_pairs={{0,8},{8,16},{16,24},{1,9},{9,17},{17,25},{2,10},{10,18},{18,26},{... | collective-permute-start | bytes 6152 | tf_op jit(solution)/shard_map/ppermute | solution.py:20
  173.9 6.5 %collective-permute-start.34 = (f32[10,10,1]{2,1,0:T(8,128)S(1)}, f32[10,10,1]{2,1,0:T(8,128)S(1)}, u32[]{:S(2)}, u32[]{:S(2)}) collective-permute-start(f32[10,10,1]{2,1,0:T(8,128)S(1)} %get-tuple-element.71), channel_id=1, source_target_pairs={{0,1},{1,2},{2,3},{4,5},{5,6},{6,7},{8,9},{9,10},{10,11},{12,13},{... | collective-permute-start | bytes 1208 | tf_op jit(solution)/shard_map/ppermute | solution.py:20
  178.5 5.8 %collective-permute-start.35 = (f32[10,10,1]{2,1,0:T(8,128)S(1)}, f32[10,10,1]{2,1,0:T(8,128)S(1)}, u32[]{:S(2)}, u32[]{:S(2)}) collective-permute-start(f32[10,10,1]{2,1,0:T(8,128)S(1)} %get-tuple-element.72), channel_id=1, source_target_pairs={{1,0},{2,1},{3,2},{5,4},{6,5},{7,6},{9,8},{10,9},{11,10},{13,12},{... | collective-permute-start | bytes 1208 | tf_op jit(solution)/shard_map/ppermute | solution.py:22
  196.9 6.6 %collective-permute-start.40 = (f32[10,10,1]{2,1,0:T(8,128)S(1)}, f32[10,10,1]{2,1,0:T(8,128)S(1)}, u32[]{:S(2)}, u32[]{:S(2)}) collective-permute-start(f32[10,10,1]{2,1,0:T(8,128)S(1)} %get-tuple-element.69), channel_id=1, source_target_pairs={{0,1},{1,2},{2,3},{4,5},{5,6},{6,7},{8,9},{9,10},{10,11},{12,13},{... | collective-permute-start | bytes 1208 | tf_op jit(solution)/shard_map/ppermute | solution.py:20
  201.6 5.8 %collective-permute-start.41 = (f32[10,10,1]{2,1,0:T(8,128)S(1)}, f32[10,10,1]{2,1,0:T(8,128)S(1)}, u32[]{:S(2)}, u32[]{:S(2)}) collective-permute-start(f32[10,10,1]{2,1,0:T(8,128)S(1)} %get-tuple-element.70), channel_id=1, source_target_pairs={{1,0},{2,1},{3,2},{5,4},{6,5},{7,6},{9,8},{10,9},{11,10},{13,12},{... | collective-permute-start | bytes 1208 | tf_op jit(solution)/shard_map/ppermute | solution.py:22
  219.4 9.7 %collective-permute-start.46 = (f32[10,10,1]{2,1,0:T(8,128)S(1)}, f32[10,10,1]{2,1,0:T(8,128)S(1)}, u32[]{:S(2)}, u32[]{:S(2)}) collective-permute-start(f32[10,10,1]{2,1,0:T(8,128)S(1)} %get-tuple-element.67), channel_id=1, source_target_pairs={{0,1},{1,2},{2,3},{4,5},{5,6},{6,7},{8,9},{9,10},{10,11},{12,13},{... | collective-permute-start | bytes 1208 | tf_op jit(solution)/shard_map/ppermute | solution.py:20
  224.1 5.8 %collective-permute-start.47 = (f32[10,10,1]{2,1,0:T(8,128)S(1)}, f32[10,10,1]{2,1,0:T(8,128)S(1)}, u32[]{:S(2)}, u32[]{:S(2)}) collective-permute-start(f32[10,10,1]{2,1,0:T(8,128)S(1)} %get-tuple-element.68), channel_id=1, source_target_pairs={{1,0},{2,1},{3,2},{5,4},{6,5},{7,6},{9,8},{10,9},{11,10},{13,12},{... | collective-permute-start | bytes 1208 | tf_op jit(solution)/shard_map/ppermute | solution.py:22
  226.0 8.6 %collective-permute-start.54 = (f32[1,4,32]{2,1,0:T(4,128)S(1)}, f32[1,4,32]{2,1,0:T(4,128)S(1)}, u32[]{:S(2)}, u32[]{:S(2)}) collective-permute-start(f32[1,4,32]{2,1,0:T(4,128)S(1)} %get-tuple-element.125), channel_id=1, source_target_pairs={{0,8},{8,16},{16,24},{1,9},{9,17},{17,25},{2,10},{10,18},{18,26},{... | collective-permute-start | bytes 1544 | tf_op jit(solution)/shard_map/ppermute | solution.py:20
  227.7 6.9 %collective-permute-start.55 = (f32[1,4,32]{2,1,0:T(4,128)S(1)}, f32[1,4,32]{2,1,0:T(4,128)S(1)}, u32[]{:S(2)}, u32[]{:S(2)}) collective-permute-start(f32[1,4,32]{2,1,0:T(4,128)S(1)} %get-tuple-element.126), channel_id=1, source_target_pairs={{8,0},{16,8},{24,16},{9,1},{17,9},{25,17},{10,2},{18,10},{26,18},{... | collective-permute-start | bytes 1544 | tf_op jit(solution)/shard_map/ppermute | solution.py:22
  230.0 7.3 %collective-permute-start.48 = (f32[1,8,64]{2,1,0:T(8,128)S(1)}, f32[1,8,64]{2,1,0:T(8,128)S(1)}, u32[]{:S(2)}, u32[]{:S(2)}) collective-permute-start(f32[1,8,64]{2,1,0:T(8,128)S(1)} %get-tuple-element.101), channel_id=1, source_target_pairs={{0,8},{8,16},{16,24},{1,9},{9,17},{17,25},{2,10},{10,18},{18,26},{... | collective-permute-start | bytes 6152 | tf_op jit(solution)/shard_map/ppermute | solution.py:20
  234.6 19.6 %collective-permute-start.56 = (f32[6,1,32]{2,1,0:T(1,128)S(1)}, f32[6,1,32]{2,1,0:T(1,128)S(1)}, u32[]{:S(2)}, u32[]{:S(2)}) collective-permute-start(f32[6,1,32]{2,1,0:T(1,128)S(1)} %get-tuple-element.119), channel_id=1, source_target_pairs={{0,4},{1,5},{2,6},{3,7},{8,12},{9,13},{10,14},{11,15},{16,20},{17,... | collective-permute-start | bytes 2312 | tf_op jit(solution)/shard_map/ppermute | solution.py:20
  236.0 18.2 %collective-permute-start.57 = (f32[6,1,32]{2,1,0:T(1,128)S(1)}, f32[6,1,32]{2,1,0:T(1,128)S(1)}, u32[]{:S(2)}, u32[]{:S(2)}) collective-permute-start(f32[6,1,32]{2,1,0:T(1,128)S(1)} %get-tuple-element.120), channel_id=1, source_target_pairs={{4,0},{5,1},{6,2},{7,3},{12,8},{13,9},{14,10},{15,11},{20,16},{21,... | collective-permute-start | bytes 2312 | tf_op jit(solution)/shard_map/ppermute | solution.py:22
  237.6 5.0 collective-permute-start.50
  245.8 8.5 %collective-permute-start.52 = (f32[10,10,1]{2,1,0:T(8,128)S(1)}, f32[10,10,1]{2,1,0:T(8,128)S(1)}, u32[]{:S(2)}, u32[]{:S(2)}) collective-permute-start(f32[10,10,1]{2,1,0:T(8,128)S(1)} %get-tuple-element.65), channel_id=1, source_target_pairs={{0,1},{1,2},{2,3},{4,5},{5,6},{6,7},{8,9},{9,10},{10,11},{12,13},{... | collective-permute-start | bytes 1208 | tf_op jit(solution)/shard_map/ppermute | solution.py:20
  252.3 5.8 %collective-permute-start.53 = (f32[10,10,1]{2,1,0:T(8,128)S(1)}, f32[10,10,1]{2,1,0:T(8,128)S(1)}, u32[]{:S(2)}, u32[]{:S(2)}) collective-permute-start(f32[10,10,1]{2,1,0:T(8,128)S(1)} %get-tuple-element.66), channel_id=1, source_target_pairs={{1,0},{2,1},{3,2},{5,4},{6,5},{7,6},{9,8},{10,9},{11,10},{13,12},{... | collective-permute-start | bytes 1208 | tf_op jit(solution)/shard_map/ppermute | solution.py:22
  259.4 10.0 %collective-permute-start.60 = (f32[1,4,32]{2,1,0:T(4,128)S(1)}, f32[1,4,32]{2,1,0:T(4,128)S(1)}, u32[]{:S(2)}, u32[]{:S(2)}) collective-permute-start(f32[1,4,32]{2,1,0:T(4,128)S(1)} %get-tuple-element.127), channel_id=1, source_target_pairs={{0,8},{8,16},{16,24},{1,9},{9,17},{17,25},{2,10},{10,18},{18,26},{... | collective-permute-start | bytes 1544 | tf_op jit(solution)/shard_map/ppermute | solution.py:20
  263.7 5.7 %collective-permute-start.61 = (f32[1,4,32]{2,1,0:T(4,128)S(1)}, f32[1,4,32]{2,1,0:T(4,128)S(1)}, u32[]{:S(2)}, u32[]{:S(2)}) collective-permute-start(f32[1,4,32]{2,1,0:T(4,128)S(1)} %get-tuple-element.128), channel_id=1, source_target_pairs={{8,0},{16,8},{24,16},{9,1},{17,9},{25,17},{10,2},{18,10},{26,18},{... | collective-permute-start | bytes 1544 | tf_op jit(solution)/shard_map/ppermute | solution.py:22
  265.1 16.9 %collective-permute-start.58 = (f32[6,6,1]{2,1,0:T(8,128)S(1)}, f32[6,6,1]{2,1,0:T(8,128)S(1)}, u32[]{:S(2)}, u32[]{:S(2)}) collective-permute-start(f32[6,6,1]{2,1,0:T(8,128)S(1)} %get-tuple-element.113), channel_id=1, source_target_pairs={{0,1},{1,2},{2,3},{4,5},{5,6},{6,7},{8,9},{9,10},{10,11},{12,13},{... | collective-permute-start | bytes 440 | tf_op jit(solution)/shard_map/ppermute | solution.py:20
  267.2 14.8 %collective-permute-start.59 = (f32[6,6,1]{2,1,0:T(8,128)S(1)}, f32[6,6,1]{2,1,0:T(8,128)S(1)}, u32[]{:S(2)}, u32[]{:S(2)}) collective-permute-start(f32[6,6,1]{2,1,0:T(8,128)S(1)} %get-tuple-element.114), channel_id=1, source_target_pairs={{1,0},{2,1},{3,2},{5,4},{6,5},{7,6},{9,8},{10,9},{11,10},{13,12},{... | collective-permute-start | bytes 440 | tf_op jit(solution)/shard_map/ppermute | solution.py:22
  275.3 7.6 %collective-permute-start.64 = (f32[6,6,1]{2,1,0:T(8,128)S(1)}, f32[6,6,1]{2,1,0:T(8,128)S(1)}, u32[]{:S(2)}, u32[]{:S(2)}) collective-permute-start(f32[6,6,1]{2,1,0:T(8,128)S(1)} %get-tuple-element.115), channel_id=1, source_target_pairs={{0,1},{1,2},{2,3},{4,5},{5,6},{6,7},{8,9},{9,10},{10,11},{12,13},{... | collective-permute-start | bytes 440 | tf_op jit(solution)/shard_map/ppermute | solution.py:20
  280.1 5.1 %collective-permute-start.65 = (f32[6,6,1]{2,1,0:T(8,128)S(1)}, f32[6,6,1]{2,1,0:T(8,128)S(1)}, u32[]{:S(2)}, u32[]{:S(2)}) collective-permute-start(f32[6,6,1]{2,1,0:T(8,128)S(1)} %get-tuple-element.116), channel_id=1, source_target_pairs={{1,0},{2,1},{3,2},{5,4},{6,5},{7,6},{9,8},{10,9},{11,10},{13,12},{... | collective-permute-start | bytes 440 | tf_op jit(solution)/shard_map/ppermute | solution.py:22
  319.8 9.5 %collective-permute-start.70 = (f32[6,6,1]{2,1,0:T(8,128)S(1)}, f32[6,6,1]{2,1,0:T(8,128)S(1)}, u32[]{:S(2)}, u32[]{:S(2)}) collective-permute-start(f32[6,6,1]{2,1,0:T(8,128)S(1)} %get-tuple-element.111), channel_id=1, source_target_pairs={{0,1},{1,2},{2,3},{4,5},{5,6},{6,7},{8,9},{9,10},{10,11},{12,13},{... | collective-permute-start | bytes 440 | tf_op jit(solution)/shard_map/ppermute | solution.py:20
  327.4 5.1 %collective-permute-start.71 = (f32[6,6,1]{2,1,0:T(8,128)S(1)}, f32[6,6,1]{2,1,0:T(8,128)S(1)}, u32[]{:S(2)}, u32[]{:S(2)}) collective-permute-start(f32[6,6,1]{2,1,0:T(8,128)S(1)} %get-tuple-element.112), channel_id=1, source_target_pairs={{1,0},{2,1},{3,2},{5,4},{6,5},{7,6},{9,8},{10,9},{11,10},{13,12},{... | collective-permute-start | bytes 440 | tf_op jit(solution)/shard_map/ppermute | solution.py:22
  367.2 9.8 %collective-permute-start.76 = (f32[10,10,1]{2,1,0:T(8,128)S(1)}, f32[10,10,1]{2,1,0:T(8,128)S(1)}, u32[]{:S(2)}, u32[]{:S(2)}) collective-permute-start(f32[10,10,1]{2,1,0:T(8,128)S(1)} %get-tuple-element.63), channel_id=1, source_target_pairs={{0,1},{1,2},{2,3},{4,5},{5,6},{6,7},{8,9},{9,10},{10,11},{12,13},{... | collective-permute-start | bytes 1208 | tf_op jit(solution)/shard_map/ppermute | solution.py:20
  375.0 5.8 %collective-permute-start.77 = (f32[10,10,1]{2,1,0:T(8,128)S(1)}, f32[10,10,1]{2,1,0:T(8,128)S(1)}, u32[]{:S(2)}, u32[]{:S(2)}) collective-permute-start(f32[10,10,1]{2,1,0:T(8,128)S(1)} %get-tuple-element.64), channel_id=1, source_target_pairs={{1,0},{2,1},{3,2},{5,4},{6,5},{7,6},{9,8},{10,9},{11,10},{13,12},{... | collective-permute-start | bytes 1208 | tf_op jit(solution)/shard_map/ppermute | solution.py:22
  392.8 6.6 %collective-permute-start.82 = (f32[10,10,1]{2,1,0:T(8,128)S(1)}, f32[10,10,1]{2,1,0:T(8,128)S(1)}, u32[]{:S(2)}, u32[]{:S(2)}) collective-permute-start(f32[10,10,1]{2,1,0:T(8,128)S(1)} %get-tuple-element.61), channel_id=1, source_target_pairs={{0,1},{1,2},{2,3},{4,5},{5,6},{6,7},{8,9},{9,10},{10,11},{12,13},{... | collective-permute-start | bytes 1208 | tf_op jit(solution)/shard_map/ppermute | solution.py:20
  397.5 5.8 %collective-permute-start.83 = (f32[10,10,1]{2,1,0:T(8,128)S(1)}, f32[10,10,1]{2,1,0:T(8,128)S(1)}, u32[]{:S(2)}, u32[]{:S(2)}) collective-permute-start(f32[10,10,1]{2,1,0:T(8,128)S(1)} %get-tuple-element.62), channel_id=1, source_target_pairs={{1,0},{2,1},{3,2},{5,4},{6,5},{7,6},{9,8},{10,9},{11,10},{13,12},{... | collective-permute-start | bytes 1208 | tf_op jit(solution)/shard_map/ppermute | solution.py:22
  416.4 6.6 %collective-permute-start.88 = (f32[10,10,1]{2,1,0:T(8,128)S(1)}, f32[10,10,1]{2,1,0:T(8,128)S(1)}, u32[]{:S(2)}, u32[]{:S(2)}) collective-permute-start(f32[10,10,1]{2,1,0:T(8,128)S(1)} %get-tuple-element.59), channel_id=1, source_target_pairs={{0,1},{1,2},{2,3},{4,5},{5,6},{6,7},{8,9},{9,10},{10,11},{12,13},{... | collective-permute-start | bytes 1208 | tf_op jit(solution)/shard_map/ppermute | solution.py:20
  421.2 5.8 %collective-permute-start.89 = (f32[10,10,1]{2,1,0:T(8,128)S(1)}, f32[10,10,1]{2,1,0:T(8,128)S(1)}, u32[]{:S(2)}, u32[]{:S(2)}) collective-permute-start(f32[10,10,1]{2,1,0:T(8,128)S(1)} %get-tuple-element.60), channel_id=1, source_target_pairs={{1,0},{2,1},{3,2},{5,4},{6,5},{7,6},{9,8},{10,9},{11,10},{13,12},{... | collective-permute-start | bytes 1208 | tf_op jit(solution)/shard_map/ppermute | solution.py:22
  438.9 6.6 %collective-permute-start.94 = (f32[10,10,1]{2,1,0:T(8,128)S(1)}, f32[10,10,1]{2,1,0:T(8,128)S(1)}, u32[]{:S(2)}, u32[]{:S(2)}) collective-permute-start(f32[10,10,1]{2,1,0:T(8,128)S(1)} %get-tuple-element.57), channel_id=1, source_target_pairs={{0,1},{1,2},{2,3},{4,5},{5,6},{6,7},{8,9},{9,10},{10,11},{12,13},{... | collective-permute-start | bytes 1208 | tf_op jit(solution)/shard_map/ppermute | solution.py:20
  443.6 5.8 %collective-permute-start.95 = (f32[10,10,1]{2,1,0:T(8,128)S(1)}, f32[10,10,1]{2,1,0:T(8,128)S(1)}, u32[]{:S(2)}, u32[]{:S(2)}) collective-permute-start(f32[10,10,1]{2,1,0:T(8,128)S(1)} %get-tuple-element.58), channel_id=1, source_target_pairs={{1,0},{2,1},{3,2},{5,4},{6,5},{7,6},{9,8},{10,9},{11,10},{13,12},{... | collective-permute-start | bytes 1208 | tf_op jit(solution)/shard_map/ppermute | solution.py:22
  455.5 4.5 collective-permute-start.97
  461.4 4.5 collective-permute-start.99
  466.1 7.8 %collective-permute-start.100 = (f32[20,20,2]{2,1,0:T(8,128)S(1)}, f32[20,20,2]{2,1,0:T(8,128)S(1)}, u32[]{:S(2)}, u32[]{:S(2)}) collective-permute-start(f32[20,20,2]{2,1,0:T(8,128)S(1)} %get-tuple-element.25), channel_id=1, source_target_pairs={{0,1},{1,2},{2,3},{4,5},{5,6},{6,7},{8,9},{9,10},{10,11},{12,13},{... | collective-permute-start | bytes 9608 | tf_op jit(solution)/shard_map/ppermute | solution.py:20
  470.8 7.5 %collective-permute-start.101 = (f32[20,20,2]{2,1,0:T(8,128)S(1)}, f32[20,20,2]{2,1,0:T(8,128)S(1)}, u32[]{:S(2)}, u32[]{:S(2)}) collective-permute-start(f32[20,20,2]{2,1,0:T(8,128)S(1)} %get-tuple-element.26), channel_id=1, source_target_pairs={{1,0},{2,1},{3,2},{5,4},{6,5},{7,6},{9,8},{10,9},{11,10},{13,12},{... | collective-permute-start | bytes 9608 | tf_op jit(solution)/shard_map/ppermute | solution.py:22
  489.1 4.5 collective-permute-start.105
  493.8 7.7 %collective-permute-start.106 = (f32[20,20,2]{2,1,0:T(8,128)S(1)}, f32[20,20,2]{2,1,0:T(8,128)S(1)}, u32[]{:S(2)}, u32[]{:S(2)}) collective-permute-start(f32[20,20,2]{2,1,0:T(8,128)S(1)} %get-tuple-element.23), channel_id=1, source_target_pairs={{0,1},{1,2},{2,3},{4,5},{5,6},{6,7},{8,9},{9,10},{10,11},{12,13},{... | collective-permute-start | bytes 9608 | tf_op jit(solution)/shard_map/ppermute | solution.py:20
  498.4 7.5 %collective-permute-start.107 = (f32[20,20,2]{2,1,0:T(8,128)S(1)}, f32[20,20,2]{2,1,0:T(8,128)S(1)}, u32[]{:S(2)}, u32[]{:S(2)}) collective-permute-start(f32[20,20,2]{2,1,0:T(8,128)S(1)} %get-tuple-element.24), channel_id=1, source_target_pairs={{1,0},{2,1},{3,2},{5,4},{6,5},{7,6},{9,8},{10,9},{11,10},{13,12},{... | collective-permute-start | bytes 9608 | tf_op jit(solution)/shard_map/ppermute | solution.py:22
  (62 other events, 1004.9 us)
